TPU v7x, 32 devices: a whole 2x2x4 slice. The times are simulated.
32 devices in a mesh: lon: 16 (over z, y, core), band: 2 (over x).
Axes of the slice: x: 2, y: 2, z: 4, core: 2. Of those that a mesh axis runs over, the one named last changes fastest.
Arguments:
- nest_field: float32 [32, 96, 9216], P(None, 'band', 'lon'), may hold values from -6 to 6
- nest_area: float32 [96, 9216], P('band', 'lon'), may hold values from 0.5 to 2
- parent_field: float32 [32, 32, 3072], P(None, 'band', 'lon'), may hold values from -6 to 6
- nest_offset: int32 [1], replicated, may hold values from 576 to 9215
- relax_rate: float32 [32], replicated, may hold values from 0.3 to 0.8
- zonal_coef: float32 [32], replicated, may hold values from 0.05 to 0.24
- merid_coef: float32 [32], replicated, may hold values from 0.05 to 0.24
Outputs:
- parent_out: float32 [32, 32, 3072], P(None, 'band', 'lon')
All inputs are finite; a program needn't handle non-finite values.
Results may differ from a plain program's by a relative error of at most 0.000084.
Values sent between devices are 32-bit elements; how exact they have to be, the bound alone decides.
No kernel may reach another device: no remote copies, remote signals or barrier semaphores. Data moves between devices by JAX's collectives and lax.ppermute only.
A program may use at most 64 MiB of HBM per device.

v0:
```python
import jax
import jax.numpy as jnp
from jax import lax
from jax.sharding import PartitionSpec as P

NS = 3


def from_behind(value, axis, steps):
    count = lax.axis_size(axis)
    pairs = [(source, (source + steps) % count) for source in range(count)]
    return lax.ppermute(value, axis, pairs)


def extended(block, sides, width, periodic):
    for axis, dim in sides:
        count = lax.axis_size(axis)
        forward = [(i, i + 1) for i in range(count - 1)]
        if periodic:
            forward.append((count - 1, 0))
        backward = [(target, source) for source, target in forward]
        low = lax.ppermute(
            lax.slice_in_dim(block, block.shape[dim] - width, None, axis=dim), axis, forward
        )
        high = lax.ppermute(lax.slice_in_dim(block, 0, width, axis=dim), axis, backward)
        block = jnp.concatenate([low, block, high], axis=dim)
    return block


def on_device(nest_field, nest_area, parent_field, nest_offset, relax_rate, zonal_coef, merid_coef):
    levels = parent_field.shape[0]
    par_rows = parent_field.shape[1]
    par_cols = parent_field.shape[2]
    nest_width = nest_field.shape[2]
    cycle_size = lax.axis_size("lon")
    offset_cells = nest_offset[0]
    stacked = jnp.concatenate([nest_field * nest_area[None], nest_area[None]], axis=0)
    row_sums = stacked.reshape(levels + 1, par_rows, 3, nest_width).sum(axis=2)
    remainder = offset_cells % 3
    start_slot = offset_cells // 3 % par_cols
    cycle_steps = offset_cells // 3 // par_cols % cycle_size
    nest_cols = jnp.arange(nest_width, dtype=jnp.int32)
    slot_ids = jnp.arange(2 * par_cols, dtype=jnp.int32)
    selector = ((nest_cols[:, None] + remainder) // 3 + start_slot == slot_ids[None, :]).astype(
        jnp.float32
    )
    compact = jnp.dot(
        row_sums.reshape((levels + 1) * par_rows, nest_width),
        selector,
        precision=lax.Precision.HIGHEST,
        preferred_element_type=jnp.float32,
    )
    compact = compact.reshape(levels + 1, par_rows, 2 * par_cols)
    own_part = compact[:, :, :par_cols]
    next_part = compact[:, :, par_cols:]
    carried = own_part + from_behind(next_part, "lon", 1)
    for bit_pos in range((cycle_size - 1).bit_length()):
        shifted = from_behind(carried, "lon", 1 << bit_pos)
        carried = jnp.where(cycle_steps >> bit_pos & 1 == 1, shifted, carried)
    restricted = carried[:levels] / carried[levels][None]
    field = parent_field + relax_rate[:, None, None] * (restricted - parent_field)
    zonal_scale = zonal_coef[:, None, None]
    merid_scale = merid_coef[:, None, None]
    for sweep in range(NS):
        padded = extended(field, (("lon", 2),), 1, True)
        field = field + zonal_scale * (padded[:, :, :-2] - 2.0 * field + padded[:, :, 2:])
        padded = extended(field, (("band", 1),), 1, False)
        field = field + merid_scale * (padded[:, :-2] - 2.0 * field + padded[:, 2:])
    return field


def solution(mesh):
    placed = (P(None, "band", "lon"), P("band", "lon"), P(None, "band", "lon"), P(), P(), P(), P())
    return jax.shard_map(
        on_device, mesh=mesh, in_specs=placed, out_specs=P(None, "band", "lon"), check_vma=False
    )
```

profile of v0, /device:TPU:0, one launch (start us, length us, event | category | flops | bytes accessed | tf_op | source)
XLA Modules:
  0.0 139.6 jit_solution(726210453062145045)
XLA Ops:
  0.7 1.0 concatenate.65
  1.7 5.3 %copy_multiply_fusion = f32[32,48,576]{2,0,1:T(8,128)} fusion(f32[32,48,576]{2,1,0:T(8,128)} %param.7, f32[48,576]{1,0:T(8,128)} %param.8), kind=kLoop, calls=%fused_computation.1 | loop fusion | flops 884736 | bytes 7188480 | tf_op jit(solution)/shard_map/mul | solution.py:37
  7.0 2.8 %maximum_reduce_fusion = f32[33,16,576]{2,0,1:T(8,128)S(1)} fusion(f32[1,16,3,576]{3,0,2,1:T(1,128)S(1)} %concatenate.65, f32[32,16,3,576]{3,0,2,1:T(8,128)} %bitcast.10), kind=kLoop, calls=%fused_computation | loop fusion | flops 1520640 | bytes 4866048 | tf_op jit(solution)/shard_map/reduce_sum | solution.py:38
  9.8 1.7 %fusion.1 = f32[33,16,384]{2,0,1:T(8,128)S(1)} fusion(f32[33,16,576]{2,0,1:T(8,128)S(1)} %maximum_reduce_fusion, s32[576]{0:T(1024)S(1)} %fusion.31), kind=kOutput, calls=%fused_computation.4 | convolution fusion | flops 1401643008 | bytes 2029824 | tf_op jit(solution)/shard_map/dot_general | solution.py:47
  11.9 0.5 collective-permute-start
  12.5 12.0 %collective-permute-done = f32[33,16,192]{2,1,0:T(8,128)S(1)} collective-permute-done((f32[33,16,192]{2,1,0:T(8,128)S(1)}, f32[33,16,192]{2,1,0:T(8,128)S(1)}, u32[]{:S(2)}, u32[]{:S(2)}) %collective-permute-start) | collective-permute-done | bytes 405536 | tf_op jit(solution)/shard_map/ppermute | solution.py:12
  24.8 11.4 %collective-permute-done.1 = f32[33,16,192]{2,1,0:T(8,128)S(1)} collective-permute-done((f32[33,16,192]{2,1,0:T(8,128)S(1)}, f32[33,16,192]{2,1,0:T(8,128)S(1)}, u32[]{:S(2)}, u32[]{:S(2)}) %collective-permute-start.1) | collective-permute-done | bytes 405536 | tf_op jit(solution)/shard_map/ppermute | solution.py:12
  36.4 12.1 %collective-permute-done.2 = f32[33,16,192]{2,1,0:T(8,128)S(1)} collective-permute-done((f32[33,16,192]{2,1,0:T(8,128)S(1)}, f32[33,16,192]{2,1,0:T(8,128)S(1)}, u32[]{:S(2)}, u32[]{:S(2)}) %collective-permute-start.2) | collective-permute-done | bytes 405536 | tf_op jit(solution)/shard_map/ppermute | solution.py:12
  48.6 11.4 %collective-permute-done.3 = f32[33,16,192]{2,1,0:T(8,128)S(1)} collective-permute-done((f32[33,16,192]{2,1,0:T(8,128)S(1)}, f32[33,16,192]{2,1,0:T(8,128)S(1)}, u32[]{:S(2)}, u32[]{:S(2)}) %collective-permute-start.3) | collective-permute-done | bytes 405536 | tf_op jit(solution)/shard_map/ppermute | solution.py:12
  60.1 0.5 collective-permute-start.4
  60.7 22.3 %collective-permute-done.4 = f32[33,16,192]{2,1,0:T(8,128)S(1)} collective-permute-done((f32[33,16,192]{2,1,0:T(8,128)S(1)}, f32[33,16,192]{2,1,0:T(8,128)S(1)}, u32[]{:S(2)}, u32[]{:S(2)}) %collective-permute-start.4) | collective-permute-done | bytes 405536 | tf_op jit(solution)/shard_map/ppermute | solution.py:12
  83.4 4.9 %collective-permute-start.6 = (f32[32,16,1]{2,1,0:T(8,128)S(1)}, f32[32,16,1]{2,1,0:T(8,128)S(1)}, u32[]{:S(2)}, u32[]{:S(2)}) collective-permute-start(f32[32,16,1]{2,1,0:T(8,128)S(1)} %get-tuple-element.18), channel_id=1, source_target_pairs={{2,0},{4,2},{6,4},{8,6},{10,8},{12,10},{14,12},{16,14},{18,16},{20... | collective-permute-start | bytes 6152 | tf_op jit(solution)/shard_map/ppermute | solution.py:25
  88.3 3.9 %collective-permute-done.6 = f32[32,16,1]{2,1,0:T(8,128)S(1)} collective-permute-done((f32[32,16,1]{2,1,0:T(8,128)S(1)}, f32[32,16,1]{2,1,0:T(8,128)S(1)}, u32[]{:S(2)}, u32[]{:S(2)}) %collective-permute-start.6) | collective-permute-done | bytes 2080 | tf_op jit(solution)/shard_map/ppermute | solution.py:25
  92.2 4.6 %collective-permute-done.5 = f32[32,16,1]{2,1,0:T(8,128)S(1)} collective-permute-done((f32[32,16,1]{2,1,0:T(8,128)S(1)}, f32[32,16,1]{2,1,0:T(8,128)S(1)}, u32[]{:S(2)}, u32[]{:S(2)}) %collective-permute-start.5) | collective-permute-done | bytes 2080 | tf_op jit(solution)/shard_map/ppermute | solution.py:22
  96.8 0.4 fusion.25
  97.3 1.3 collective-permute-start.8
  98.6 4.6 %collective-permute-start.7 = (f32[32,1,192]{2,1,0:T(1,128)S(1)}, f32[32,1,192]{2,1,0:T(1,128)S(1)}, u32[]{:S(2)}, u32[]{:S(2)}) collective-permute-start(f32[32,1,192]{2,1,0:T(1,128)S(1)} %get-tuple-element.15), channel_id=1, source_target_pairs={{0,1},{2,3},{4,5},{6,7},{8,9},{10,11},{12,13},{14,15},{16,17},{18,... | collective-permute-start | bytes 73736 | tf_op jit(solution)/shard_map/ppermute | solution.py:22
  103.1 1.6 %collective-permute-done.7 = f32[32,1,192]{2,1,0:T(1,128)S(1)} collective-permute-done((f32[32,1,192]{2,1,0:T(1,128)S(1)}, f32[32,1,192]{2,1,0:T(1,128)S(1)}, u32[]{:S(2)}, u32[]{:S(2)}) %collective-permute-start.7) | collective-permute-done | bytes 24608 | tf_op jit(solution)/shard_map/ppermute | solution.py:22
  105.2 0.5 collective-permute-start.9
  105.6 3.4 %collective-permute-done.10 = f32[32,16,1]{2,1,0:T(8,128)S(1)} collective-permute-done((f32[32,16,1]{2,1,0:T(8,128)S(1)}, f32[32,16,1]{2,1,0:T(8,128)S(1)}, u32[]{:S(2)}, u32[]{:S(2)}) %collective-permute-start.10) | collective-permute-done | bytes 2080 | tf_op jit(solution)/shard_map/ppermute | solution.py:25
  109.0 4.7 %collective-permute-done.9 = f32[32,16,1]{2,1,0:T(8,128)S(1)} collective-permute-done((f32[32,16,1]{2,1,0:T(8,128)S(1)}, f32[32,16,1]{2,1,0:T(8,128)S(1)}, u32[]{:S(2)}, u32[]{:S(2)}) %collective-permute-start.9) | collective-permute-done | bytes 2080 | tf_op jit(solution)/shard_map/ppermute | solution.py:22
  113.7 0.4 fusion.17
  114.2 1.3 collective-permute-start.12
  115.5 4.5 %collective-permute-start.11 = (f32[32,1,192]{2,1,0:T(1,128)S(1)}, f32[32,1,192]{2,1,0:T(1,128)S(1)}, u32[]{:S(2)}, u32[]{:S(2)}) collective-permute-start(f32[32,1,192]{2,1,0:T(1,128)S(1)} %get-tuple-element.11), channel_id=1, source_target_pairs={{0,1},{2,3},{4,5},{6,7},{8,9},{10,11},{12,13},{14,15},{16,17},{18,... | collective-permute-start | bytes 73736 | tf_op jit(solution)/shard_map/ppermute | solution.py:22
  120.1 1.6 %collective-permute-done.11 = f32[32,1,192]{2,1,0:T(1,128)S(1)} collective-permute-done((f32[32,1,192]{2,1,0:T(1,128)S(1)}, f32[32,1,192]{2,1,0:T(1,128)S(1)}, u32[]{:S(2)}, u32[]{:S(2)}) %collective-permute-start.11) | collective-permute-done | bytes 24608 | tf_op jit(solution)/shard_map/ppermute | solution.py:22
  122.1 0.5 collective-permute-start.13
  122.6 3.4 %collective-permute-done.14 = f32[32,16,1]{2,1,0:T(8,128)S(1)} collective-permute-done((f32[32,16,1]{2,1,0:T(8,128)S(1)}, f32[32,16,1]{2,1,0:T(8,128)S(1)}, u32[]{:S(2)}, u32[]{:S(2)}) %collective-permute-start.14) | collective-permute-done | bytes 2080 | tf_op jit(solution)/shard_map/ppermute | solution.py:25
  125.9 4.7 %collective-permute-done.13 = f32[32,16,1]{2,1,0:T(8,128)S(1)} collective-permute-done((f32[32,16,1]{2,1,0:T(8,128)S(1)}, f32[32,16,1]{2,1,0:T(8,128)S(1)}, u32[]{:S(2)}, u32[]{:S(2)}) %collective-permute-start.13) | collective-permute-done | bytes 2080 | tf_op jit(solution)/shard_map/ppermute | solution.py:22
  131.1 1.3 collective-permute-start.16
  132.4 4.5 %collective-permute-start.15 = (f32[32,1,192]{2,1,0:T(1,128)S(1)}, f32[32,1,192]{2,1,0:T(1,128)S(1)}, u32[]{:S(2)}, u32[]{:S(2)}) collective-permute-start(f32[32,1,192]{2,1,0:T(1,128)S(1)} %get-tuple-element.7), channel_id=1, source_target_pairs={{0,1},{2,3},{4,5},{6,7},{8,9},{10,11},{12,13},{14,15},{16,17},{18,... | collective-permute-start | bytes 73736 | tf_op jit(solution)/shard_map/ppermute | solution.py:22
  137.0 1.6 %collective-permute-done.15 = f32[32,1,192]{2,1,0:T(1,128)S(1)} collective-permute-done((f32[32,1,192]{2,1,0:T(1,128)S(1)}, f32[32,1,192]{2,1,0:T(1,128)S(1)}, u32[]{:S(2)}, u32[]{:S(2)}) %collective-permute-start.15) | collective-permute-done | bytes 24608 | tf_op jit(solution)/shard_map/ppermute | solution.py:22
  138.5 1.0 fusion.5
  (36 shorter events, 2.9 us)
Async XLA Ops:
  11.9 12.6 %collective-permute-start = (f32[33,16,192]{2,1,0:T(8,128)S(1)}, f32[33,16,192]{2,1,0:T(8,128)S(1)}, u32[]{:S(2)}, u32[]{:S(2)}) collective-permute-start(f32[33,16,192]{2,1,0:T(8,128)S(1)} %copy.16), channel_id=1, source_target_pairs={{0,2},{2,4},{4,6},{6,8},{8,10},{10,12},{12,14},{14,16},{16,18},{18... | collective-permute-start | bytes 1216520 | tf_op jit(solution)/shard_map/ppermute | solution.py:12
  24.5 58.6 %copy-start = (f32[32,16,192]{2,1,0:T(8,128)S(1)}, f32[32,16,192]{2,1,0:T(8,128)}, u32[]{:S(2)}) copy-start(f32[32,16,192]{2,1,0:T(8,128)} %param.9) | copy-start | bytes 1179652
  24.5 58.6 %copy-start.3 = (f32[32]{0:T(128)S(1)}, f32[32]{0:T(128)}, u32[]{:S(2)}) copy-start(f32[32]{0:T(128)} %param.11) | copy-start | bytes 388
  24.7 11.5 %collective-permute-start.1 = (f32[33,16,192]{2,1,0:T(8,128)S(1)}, f32[33,16,192]{2,1,0:T(8,128)S(1)}, u32[]{:S(2)}, u32[]{:S(2)}) collective-permute-start(f32[33,16,192]{2,1,0:T(8,128)S(1)} %copy_add_fusion), channel_id=1, source_target_pairs={{0,2},{2,4},{4,6},{6,8},{8,10},{10,12},{12,14},{14,16},{16,18},{18... | collective-permute-start | bytes 1216520 | tf_op jit(solution)/shard_map/ppermute | solution.py:12
  36.3 60.5 %copy-start.1 = (f32[32]{0:T(128)S(1)}, f32[32]{0:T(128)}, u32[]{:S(2)}) copy-start(f32[32]{0:T(128)} %param.12) | copy-start | bytes 388
  36.3 12.2 %collective-permute-start.2 = (f32[33,16,192]{2,1,0:T(8,128)S(1)}, f32[33,16,192]{2,1,0:T(8,128)S(1)}, u32[]{:S(2)}, u32[]{:S(2)}) collective-permute-start(f32[33,16,192]{2,1,0:T(8,128)S(1)} %broadcast_select_fusion), channel_id=1, source_target_pairs={{0,4},{2,6},{4,8},{6,10},{8,12},{10,14},{12,16},{14,18},{16,20},{1... | collective-permute-start | bytes 1216520 | tf_op jit(solution)/shard_map/ppermute | solution.py:12
  48.6 56.2 %copy-start.2 = (f32[32]{0:T(128)S(1)}, f32[32]{0:T(128)}, u32[]{:S(2)}) copy-start(f32[32]{0:T(128)} %param.13) | copy-start | bytes 388
  48.6 11.5 %collective-permute-start.3 = (f32[33,16,192]{2,1,0:T(8,128)S(1)}, f32[33,16,192]{2,1,0:T(8,128)S(1)}, u32[]{:S(2)}, u32[]{:S(2)}) collective-permute-start(f32[33,16,192]{2,1,0:T(8,128)S(1)} %broadcast_select_fusion.1), channel_id=1, source_target_pairs={{0,8},{2,10},{4,12},{6,14},{8,16},{10,18},{12,20},{14,22},{16,24},... | collective-permute-start | bytes 1216520 | tf_op jit(solution)/shard_map/ppermute | solution.py:12
  60.1 22.8 %collective-permute-start.4 = (f32[33,16,192]{2,1,0:T(8,128)S(1)}, f32[33,16,192]{2,1,0:T(8,128)S(1)}, u32[]{:S(2)}, u32[]{:S(2)}) collective-permute-start(f32[33,16,192]{2,1,0:T(8,128)S(1)} %broadcast_select_fusion.2), channel_id=1, source_target_pairs={{0,16},{2,18},{4,20},{6,22},{8,24},{10,26},{12,28},{14,30},{16,0},... | collective-permute-start | bytes 1216520 | tf_op jit(solution)/shard_map/ppermute | solution.py:12
  83.4 8.8 %collective-permute-start.6 = (f32[32,16,1]{2,1,0:T(8,128)S(1)}, f32[32,16,1]{2,1,0:T(8,128)S(1)}, u32[]{:S(2)}, u32[]{:S(2)}) collective-permute-start(f32[32,16,1]{2,1,0:T(8,128)S(1)} %get-tuple-element.18), channel_id=1, source_target_pairs={{2,0},{4,2},{6,4},{8,6},{10,8},{12,10},{14,12},{16,14},{18,16},{20... | collective-permute-start | bytes 6152 | tf_op jit(solution)/shard_map/ppermute | solution.py:25
  88.3 8.5 %collective-permute-start.5 = (f32[32,16,1]{2,1,0:T(8,128)S(1)}, f32[32,16,1]{2,1,0:T(8,128)S(1)}, u32[]{:S(2)}, u32[]{:S(2)}) collective-permute-start(f32[32,16,1]{2,1,0:T(8,128)S(1)} %get-tuple-element.17), channel_id=1, source_target_pairs={{0,2},{2,4},{4,6},{6,8},{8,10},{10,12},{12,14},{14,16},{16,18},{18... | collective-permute-start | bytes 6152 | tf_op jit(solution)/shard_map/ppermute | solution.py:22
  97.3 5.9 %collective-permute-start.8 = (f32[32,1,192]{2,1,0:T(1,128)S(1)}, f32[32,1,192]{2,1,0:T(1,128)S(1)}, u32[]{:S(2)}, u32[]{:S(2)}) collective-permute-start(f32[32,1,192]{2,1,0:T(1,128)S(1)} %get-tuple-element.16), channel_id=1, source_target_pairs={{1,0},{3,2},{5,4},{7,6},{9,8},{11,10},{13,12},{15,14},{17,16},{19,... | collective-permute-start | bytes 73736 | tf_op jit(solution)/shard_map/ppermute | solution.py:25
  98.6 6.1 %collective-permute-start.7 = (f32[32,1,192]{2,1,0:T(1,128)S(1)}, f32[32,1,192]{2,1,0:T(1,128)S(1)}, u32[]{:S(2)}, u32[]{:S(2)}) collective-permute-start(f32[32,1,192]{2,1,0:T(1,128)S(1)} %get-tuple-element.15), channel_id=1, source_target_pairs={{0,1},{2,3},{4,5},{6,7},{8,9},{10,11},{12,13},{14,15},{16,17},{18,... | collective-permute-start | bytes 73736 | tf_op jit(solution)/shard_map/ppermute | solution.py:22
  105.1 3.9 %collective-permute-start.10 = (f32[32,16,1]{2,1,0:T(8,128)S(1)}, f32[32,16,1]{2,1,0:T(8,128)S(1)}, u32[]{:S(2)}, u32[]{:S(2)}) collective-permute-start(f32[32,16,1]{2,1,0:T(8,128)S(1)} %get-tuple-element.14), channel_id=1, source_target_pairs={{2,0},{4,2},{6,4},{8,6},{10,8},{12,10},{14,12},{16,14},{18,16},{20... | collective-permute-start | bytes 6152 | tf_op jit(solution)/shard_map/ppermute | solution.py:25
  105.2 8.5 %collective-permute-start.9 = (f32[32,16,1]{2,1,0:T(8,128)S(1)}, f32[32,16,1]{2,1,0:T(8,128)S(1)}, u32[]{:S(2)}, u32[]{:S(2)}) collective-permute-start(f32[32,16,1]{2,1,0:T(8,128)S(1)} %get-tuple-element.13), channel_id=1, source_target_pairs={{0,2},{2,4},{4,6},{6,8},{8,10},{10,12},{12,14},{14,16},{16,18},{18... | collective-permute-start | bytes 6152 | tf_op jit(solution)/shard_map/ppermute | solution.py:22
  114.2 5.9 %collective-permute-start.12 = (f32[32,1,192]{2,1,0:T(1,128)S(1)}, f32[32,1,192]{2,1,0:T(1,128)S(1)}, u32[]{:S(2)}, u32[]{:S(2)}) collective-permute-start(f32[32,1,192]{2,1,0:T(1,128)S(1)} %get-tuple-element.12), channel_id=1, source_target_pairs={{1,0},{3,2},{5,4},{7,6},{9,8},{11,10},{13,12},{15,14},{17,16},{19,... | collective-permute-start | bytes 73736 | tf_op jit(solution)/shard_map/ppermute | solution.py:25
  115.5 6.1 %collective-permute-start.11 = (f32[32,1,192]{2,1,0:T(1,128)S(1)}, f32[32,1,192]{2,1,0:T(1,128)S(1)}, u32[]{:S(2)}, u32[]{:S(2)}) collective-permute-start(f32[32,1,192]{2,1,0:T(1,128)S(1)} %get-tuple-element.11), channel_id=1, source_target_pairs={{0,1},{2,3},{4,5},{6,7},{8,9},{10,11},{12,13},{14,15},{16,17},{18,... | collective-permute-start | bytes 73736 | tf_op jit(solution)/shard_map/ppermute | solution.py:22
  122.0 3.9 %collective-permute-start.14 = (f32[32,16,1]{2,1,0:T(8,128)S(1)}, f32[32,16,1]{2,1,0:T(8,128)S(1)}, u32[]{:S(2)}, u32[]{:S(2)}) collective-permute-start(f32[32,16,1]{2,1,0:T(8,128)S(1)} %get-tuple-element.10), channel_id=1, source_target_pairs={{2,0},{4,2},{6,4},{8,6},{10,8},{12,10},{14,12},{16,14},{18,16},{20... | collective-permute-start | bytes 6152 | tf_op jit(solution)/shard_map/ppermute | solution.py:25
  122.1 8.5 %collective-permute-start.13 = (f32[32,16,1]{2,1,0:T(8,128)S(1)}, f32[32,16,1]{2,1,0:T(8,128)S(1)}, u32[]{:S(2)}, u32[]{:S(2)}) collective-permute-start(f32[32,16,1]{2,1,0:T(8,128)S(1)} %get-tuple-element.9), channel_id=1, source_target_pairs={{0,2},{2,4},{4,6},{6,8},{8,10},{10,12},{12,14},{14,16},{16,18},{18... | collective-permute-start | bytes 6152 | tf_op jit(solution)/shard_map/ppermute | solution.py:22
  131.1 5.9 %collective-permute-start.16 = (f32[32,1,192]{2,1,0:T(1,128)S(1)}, f32[32,1,192]{2,1,0:T(1,128)S(1)}, u32[]{:S(2)}, u32[]{:S(2)}) collective-permute-start(f32[32,1,192]{2,1,0:T(1,128)S(1)} %get-tuple-element.8), channel_id=1, source_target_pairs={{1,0},{3,2},{5,4},{7,6},{9,8},{11,10},{13,12},{15,14},{17,16},{19,... | collective-permute-start | bytes 73736 | tf_op jit(solution)/shard_map/ppermute | solution.py:25
  132.4 6.1 %collective-permute-start.15 = (f32[32,1,192]{2,1,0:T(1,128)S(1)}, f32[32,1,192]{2,1,0:T(1,128)S(1)}, u32[]{:S(2)}, u32[]{:S(2)}) collective-permute-start(f32[32,1,192]{2,1,0:T(1,128)S(1)} %get-tuple-element.7), channel_id=1, source_target_pairs={{0,1},{2,3},{4,5},{6,7},{8,9},{10,11},{12,13},{14,15},{16,17},{18,... | collective-permute-start | bytes 73736 | tf_op jit(solution)/shard_map/ppermute | solution.py:22
where the time goes:
time: 140 us
  waiting for transfers between devices  98.5 us (70%)
  starting transfers between devices  24.8 us (18%)
  other arithmetic  11.5 us (8%)
  local copies, waits for them, and re-layouts  1.99 us (1%)
  matrix products  1.71 us (1%)
    ppermute x5, waiting for transfers between devices, from_behind(): return lax.ppermute(value, axis, pairs)  69.2 us
    ppermute x6, waiting for transfers between devices, extended(): lax.ppermute(lax.slice_in_dim(block, block.shape[dim] - width, None, axis...  18.6 us
    ppermute x6, starting transfers between devices, extended(): lax.ppermute(lax.slice_in_dim(block, block.shape[dim] - width, None, axis...  14.6 us
    ppermute x6, waiting for transfers between devices, extended(): lax.ppermute(lax.slice_in_dim(block, 0, width, axis=dim), axis, backward)  10.7 us
    ppermute x6, starting transfers between devices, extended(): lax.ppermute(lax.slice_in_dim(block, 0, width, axis=dim), axis, backward)  8.91 us
    mul x1, other arithmetic, on_device(): nest_field * nest_area[None]  5.25 us
  transfers between devices with their start and end apart: 17, of which 14 were waited for; matrix products, arithmetic and copies ran while one was open for 0% of the time, Pallas kernels for 0%

commit v1 on v0

v1 whole, which is shorter than its diff:
```python
import functools

import jax
import jax.numpy as jnp
from jax import lax
from jax.experimental import pallas as pl
from jax.experimental.pallas import tpu as pltpu
from jax.sharding import PartitionSpec as P

NS = 3
HALO = 4
LANE = 128
SUB = 8


def lane_blocks(width):
    return -(-width // LANE)


def split_dot(value, selector, parts):
    total = None
    for part in range(parts):
        piece = value.astype(jnp.bfloat16)
        term = jnp.dot(piece, selector, preferred_element_type=jnp.float32)
        total = term if total is None else total + term
        if part + 1 < parts:
            value = value - piece.astype(jnp.float32)
    return total


def restrict_kernel(
    offset_ref, *refs, blocks, nest_width, par_cols, par_rows, frame, level_block, pad_cols
):
    field_refs = refs[:blocks]
    area_refs = refs[blocks : 2 * blocks]
    near_ref, far_ref, before_ref, after_ref, sel_ref, stage_ref = refs[2 * blocks :]
    step = pl.program_id(0)
    offset = offset_ref[0]
    remainder = offset % 3
    place = offset // 3 % par_cols + HALO
    tile = place // SUB
    rows = level_block * par_rows

    def weights(i):
        out = []
        for b in range(blocks):
            a = area_refs[b][pl.ds(i, par_rows, stride=3), :]
            if (b + 1) * LANE > nest_width:
                lanes = lax.broadcasted_iota(jnp.int32, a.shape, 1) + b * LANE
                a = jnp.where(lanes < nest_width, a, 0.0)
            out.append(a)
        return out

    area_at = [weights(i) for i in range(3)]

    @pl.when(step == 0)
    def _():
        g = lax.broadcasted_iota(jnp.int32, (blocks * LANE, pad_cols), 0)
        c = lax.broadcasted_iota(jnp.int32, (blocks * LANE, pad_cols), 1)
        low = 3 * (c - place % SUB) - remainder
        hit = (g >= low) & (g < low + 3) & (g < nest_width)
        sel_ref[...] = jnp.where(hit, 1.0, 0.0).astype(jnp.bfloat16)
        stage_ref[...] = jnp.zeros_like(stage_ref)

        total = jnp.concatenate(
            [area_at[0][b] + area_at[1][b] + area_at[2][b] for b in range(blocks)], axis=1
        )
        compact = split_dot(total, sel_ref[...], 3)
        wide = jnp.concatenate([compact, jnp.zeros_like(compact)], axis=1)
        lanes = lax.broadcasted_iota(jnp.int32, (par_rows, pad_cols), 1)

        def packed(shift):
            moved = pltpu.roll(wide, (tile * SUB + shift + 2 * pad_cols) % (2 * pad_cols), 1)
            part = jnp.where(lanes < frame, moved[:, :pad_cols], 0.0)
            return part

        def put(ref, row, part):
            half = SUB
            pieces = [part[k * half : (k + 1) * half] for k in range(par_rows // half)]
            for k, piece in enumerate(pieces):
                ref[row : row + SUB, k * pad_cols : (k + 1) * pad_cols] = piece

        put(near_ref, frame, packed(0))
        put(far_ref, 0, packed(-par_cols))
        edge = lanes >= par_cols
        put(before_ref, SUB, jnp.where(edge & (tile == 0), packed(par_cols), 0.0))
        last = tile == par_cols // SUB
        put(after_ref, 0, jnp.where((lanes < SUB) & last, packed(-2 * par_cols), 0.0))

    sums = []
    for b in range(blocks):
        acc = None
        for i in range(3):
            f = field_refs[b][:, pl.ds(i, par_rows, stride=3), :]
            if (b + 1) * LANE > nest_width:
                lanes = lax.broadcasted_iota(jnp.int32, f.shape, 2) + b * LANE
                f = jnp.where(lanes < nest_width, f, 0.0)
            term = f * area_at[i][b][None]
            acc = term if acc is None else acc + term
        sums.append(acc.reshape(rows, LANE))
    compact = split_dot(jnp.concatenate(sums, axis=1), sel_ref[...], 2)
    turned = compact.T
    stage_ref[pl.ds(pl.multiple_of(tile * SUB, SUB), frame), :] = turned[:frame]
    near_ref[:frame, pl.ds(pl.multiple_of(step * rows, LANE), rows)] = stage_ref[:frame, :]
    far_ref[SUB:, pl.ds(pl.multiple_of(step * rows, LANE), rows)] = stage_ref[
        par_cols : par_cols + frame, :
    ]
    before_ref[:SUB, pl.ds(pl.multiple_of(step * rows, LANE), rows)] = stage_ref[:SUB, :]
    after_ref[SUB:, pl.ds(pl.multiple_of(step * rows, LANE), rows)] = stage_ref[
        2 * par_cols : 2 * par_cols + SUB, :
    ]


def restrict(nest_field, nest_area, nest_offset, par_cols):
    levels, nest_rows, nest_width = nest_field.shape
    par_rows = nest_rows // 3
    frame = par_cols + 2 * HALO
    pad_cols = lane_blocks(frame) * LANE
    blocks = lane_blocks(nest_width)
    level_block = LANE // par_rows
    span = levels * par_rows
    rows = level_block * par_rows
    field_specs = [
        pl.BlockSpec((level_block, nest_rows, LANE), functools.partial(lambda b, s, o: (s, 0, b), b))
        for b in range(blocks)
    ]
    area_specs = [
        pl.BlockSpec((nest_rows, LANE), functools.partial(lambda b, s, o: (0, b), b))
        for b in range(blocks)
    ]

    def whole(count):
        return pl.BlockSpec((count, span), lambda s, o: (0, 0))

    sizes = (frame + SUB, frame + SUB, 2 * SUB, 2 * SUB)
    return pl.pallas_call(
        functools.partial(
            restrict_kernel,
            blocks=blocks,
            nest_width=nest_width,
            par_cols=par_cols,
            par_rows=par_rows,
            frame=frame,
            level_block=level_block,
            pad_cols=pad_cols,
        ),
        grid_spec=pltpu.PrefetchScalarGridSpec(
            num_scalar_prefetch=1,
            grid=(levels // level_block,),
            in_specs=field_specs + area_specs,
            out_specs=[whole(n) for n in sizes],
            scratch_shapes=[
                pltpu.VMEM((blocks * LANE, pad_cols), jnp.bfloat16),
                pltpu.VMEM((2 * par_cols + SUB, rows), jnp.float32),
            ],
        ),
        out_shape=[jax.ShapeDtypeStruct((n, span), jnp.float32) for n in sizes],
        compiler_params=pltpu.CompilerParams(dimension_semantics=("arbitrary",)),
        name="restrict",
    )(nest_offset, *([nest_field] * blocks), *([nest_area] * blocks))


def edges_kernel(left_ref, right_ref, first_ref, last_ref, *, par_cols):
    span = first_ref.shape[1]
    first_ref[...] = left_ref[...].reshape(span, LANE).T[:SUB]
    low = (par_cols - SUB) % LANE
    last_ref[...] = right_ref[...].reshape(span, LANE).T[low : low + SUB]


def parent_edges(parent):
    levels, par_rows, par_cols = parent.shape
    span = levels * par_rows
    block = (levels, par_rows, LANE)
    last = (par_cols - SUB) // LANE
    return pl.pallas_call(
        functools.partial(edges_kernel, par_cols=par_cols),
        grid=(1,),
        in_specs=[
            pl.BlockSpec(block, lambda i: (0, 0, 0)),
            pl.BlockSpec(block, lambda i: (0, 0, last)),
        ],
        out_specs=[pl.BlockSpec((SUB, span), lambda i: (0, 0))] * 2,
        out_shape=[jax.ShapeDtypeStruct((SUB, span), jnp.float32)] * 2,
        name="edges",
    )(parent, parent)


def zonal_kernel(
    relax_ref, zonal_ref, band_ref, near_ref, far_ref, low_ref, high_ref, parent_ref,
    out_ref, *rest, frame, par_cols, par_rows, levels, pad_cols, starts
):
    edge_refs = rest[: len(starts)]
    num_ref, hal_ref, own_ref, *z_refs = rest[len(starts) :]
    span = levels * par_rows
    tall = pad_cols
    num = near_ref[:frame, :] + far_ref[SUB:, :]
    num = jnp.concatenate([num, jnp.zeros((tall - frame, span), jnp.float32)], axis=0)
    num_ref[...] = num.T
    halo = jnp.concatenate(
        [low_ref[...], high_ref[...], jnp.zeros((LANE - 2 * SUB, span), jnp.float32)], axis=0
    )
    hal_ref[...] = halo.T
    packed = near_ref[frame:, :] + far_ref[:SUB, :]
    area = jnp.concatenate(
        [packed[:, k * pad_cols : (k + 1) * pad_cols] for k in range(par_rows // SUB)], axis=0
    )
    inverse = 1.0 / area
    lanes = lax.broadcasted_iota(jnp.int32, (par_rows, pad_cols), 1)
    own_ref[...] = jnp.zeros_like(own_ref)
    own_ref[:, :, :par_cols] = parent_ref[...]

    def body(level, carry):
        at = pl.multiple_of(level * par_rows, par_rows)
        halo = hal_ref[pl.ds(at, par_rows), :]
        if pad_cols > LANE:
            halo = jnp.concatenate(
                [halo, jnp.zeros((par_rows, pad_cols - LANE), jnp.float32)], axis=1
            )
        own = pltpu.roll(own_ref[level], HALO, 1)
        parent = jnp.where(
            lanes < HALO,
            pltpu.roll(halo, pad_cols - HALO, 1),
            jnp.where(
                lanes < par_cols + HALO, own, pltpu.roll(halo, par_cols + HALO - SUB, 1)
            ),
        )
        restricted = num_ref[pl.ds(at, par_rows), :] * inverse
        field = parent + relax_ref[level] * (restricted - parent)
        coef = zonal_ref[level]
        for _ in range(NS):
            sides = pltpu.roll(field, 1, 1) + pltpu.roll(field, pad_cols - 1, 1)
            field = field + coef * (sides - 2.0 * field)
        field = pltpu.roll(field, pad_cols - HALO, 1)
        out_ref[level] = field[:, :par_cols]
        for k, z_ref in enumerate(z_refs):
            z_ref[pl.ds(at, par_rows), :] = field[:, k * LANE : (k + 1) * LANE]
        return carry

    lax.fori_loop(0, levels, body, 0, unroll=4)
    for edge_ref, (fixed, by_band) in zip(edge_refs, starts):
        for i in range(NS):
            start = fixed + i + (by_band * band_ref[0] if by_band else 0)
            for k, z_ref in enumerate(z_refs):
                edge_ref[i * levels : (i + 1) * levels, k * LANE : (k + 1) * LANE] = z_ref[
                    pl.ds(start, levels, stride=par_rows), :
                ]


def zonal(relax, coef, band, near, far, low, high, parent, starts):
    levels, par_rows, par_cols = parent.shape
    frame = par_cols + 2 * HALO
    pad_cols = lane_blocks(frame) * LANE
    wide = lane_blocks(par_cols)
    span = levels * par_rows
    smem = pl.BlockSpec(memory_space=pltpu.SMEM)
    vmem = pl.BlockSpec(memory_space=pltpu.VMEM)
    edge = jax.ShapeDtypeStruct((NS * levels, wide * LANE), jnp.float32)
    return pl.pallas_call(
        functools.partial(
            zonal_kernel,
            frame=frame,
            par_cols=par_cols,
            par_rows=par_rows,
            levels=levels,
            pad_cols=pad_cols,
            starts=starts,
        ),
        in_specs=[smem] * 3 + [vmem] * 5,
        out_specs=[vmem] * (1 + len(starts)),
        out_shape=[jax.ShapeDtypeStruct(parent.shape, jnp.float32)] + [edge] * len(starts),
        scratch_shapes=[
            pltpu.VMEM((span, pad_cols), jnp.float32),
            pltpu.VMEM((span, LANE), jnp.float32),
            pltpu.VMEM((levels, par_rows, pad_cols), jnp.float32),
        ]
        + [pltpu.VMEM((span, LANE), jnp.float32)] * wide,
        name="zonal",
    )(relax, coef, band, near, far, low, high, parent)


def merid_kernel(
    coef_ref, flag_ref, field_ref, before_ref, after_ref, out_ref, *halo_refs,
    levels, par_rows, par_cols
):
    wide = len(halo_refs) // 2
    keep_before = flag_ref[0].astype(jnp.float32)
    keep_after = flag_ref[1].astype(jnp.float32)
    for k in range(wide):
        for i in range(NS):
            rows = slice(i * levels, (i + 1) * levels)
            cols = slice(k * LANE, (k + 1) * LANE)
            halo_refs[k][pl.ds(SUB - NS + i, levels, stride=SUB), :] = before_ref[rows, cols]
            halo_refs[wide + k][pl.ds(i, levels, stride=SUB), :] = after_ref[rows, cols]

    def body(level, carry):
        at = pl.multiple_of(level * SUB, SUB)
        before = jnp.concatenate([halo_refs[k][pl.ds(at, SUB), :] for k in range(wide)], axis=1)
        after = jnp.concatenate(
            [halo_refs[wide + k][pl.ds(at, SUB), :] for k in range(wide)], axis=1
        )
        mine = jnp.concatenate(
            [
                field_ref[level],
                jnp.zeros((par_rows, wide * LANE - par_cols), jnp.float32),
            ],
            axis=1,
        ) if wide * LANE > par_cols else field_ref[level]
        row = lax.broadcasted_iota(jnp.int32, (par_rows + 2 * SUB, wide * LANE), 0)
        mask = jnp.where(
            row < SUB, keep_before, jnp.where(row < SUB + par_rows, 1.0, keep_after)
        )
        count = par_rows + 2 * SUB
        good = (row >= SUB - NS) & (row < SUB + par_rows + NS)
        field = jnp.where(good, jnp.concatenate([before, mine, after], axis=0), 0.0) * mask
        coef = coef_ref[level]
        for _ in range(NS):
            sides = pltpu.roll(field, 1, 0) + pltpu.roll(field, count - 1, 0)
            field = (field + coef * (sides - 2.0 * field)) * mask
        out_ref[level] = field[SUB : SUB + par_rows, :par_cols]
        return carry

    lax.fori_loop(0, levels, body, 0, unroll=4)


def merid(coef, flags, field, before, after):
    levels, par_rows, par_cols = field.shape
    wide = lane_blocks(par_cols)
    smem = pl.BlockSpec(memory_space=pltpu.SMEM)
    vmem = pl.BlockSpec(memory_space=pltpu.VMEM)
    return pl.pallas_call(
        functools.partial(merid_kernel, levels=levels, par_rows=par_rows, par_cols=par_cols),
        in_specs=[smem] * 2 + [vmem] * 3,
        out_specs=vmem,
        out_shape=jax.ShapeDtypeStruct(field.shape, jnp.float32),
        scratch_shapes=[pltpu.VMEM((levels * SUB, LANE), jnp.float32)] * (2 * wide),
        name="merid",
    )(coef, flags, field, before, after)


def turn(value, steps):
    count = lax.axis_size("lon")
    return lax.ppermute(value, "lon", [(i, (i + steps) % count) for i in range(count)])


def bins_of(frame):
    quantum = 5 * SUB
    return quantum, -(-frame // quantum)


def on_device(nest_field, nest_area, parent_field, nest_offset, relax_rate, zonal_coef, merid_coef):
    par_cols = parent_field.shape[2]
    par_rows = parent_field.shape[1]
    frame = par_cols + 2 * HALO
    cycle = lax.axis_size("lon")
    bands = lax.axis_size("band")
    band = lax.axis_index("band").astype(jnp.int32)

    first, last = parent_edges(parent_field)
    low = turn(last, 1)
    high = turn(first, -1)
    near, far, before, after = restrict(nest_field, nest_area, nest_offset, par_cols)

    quantum, bins = bins_of(frame)
    places = nest_offset[0] // 3
    steps = places // par_cols % cycle
    slot = (places % par_cols + HALO) // quantum

    def branch(step, number):
        start = number * quantum
        count = min(start + quantum, frame)

        def send(near, far, before, after):
            got_near = turn(near[start:], step)
            got_far = turn(far[: SUB + count], step + 1)
            got_near = jnp.pad(got_near, ((start, 0), (0, 0)))
            got_far = jnp.pad(got_far, ((0, frame - count), (0, 0)))
            if number == 0:
                got_near = got_near.at[par_cols + 2 * HALO - SUB :].add(turn(before, step - 1))
            if number == bins - 1:
                got_far = got_far.at[: 2 * SUB].add(turn(after, step + 2))
            return got_near, got_far

        return send

    branches = [branch(step, number) for step in range(cycle) for number in range(bins)]
    near, far = lax.switch(steps * bins + slot, branches, near, far, before, after)

    if bands == 2:
        starts = ((par_rows - NS, -(par_rows - NS)),)
    else:
        starts = ((par_rows - NS, 0), (0, 0))
    field, *edges = zonal(
        relax_rate, zonal_coef, band[None], near, far, low, high, parent_field, starts
    )
    if bands == 2:
        other = lax.ppermute(edges[0], "band", [(0, 1), (1, 0)])
        north, south = other, other
    else:
        north = lax.ppermute(edges[0], "band", [(i, i + 1) for i in range(bands - 1)])
        south = lax.ppermute(edges[1], "band", [(i + 1, i) for i in range(bands - 1)])
    flags = jnp.stack([band > 0, band < bands - 1]).astype(jnp.int32)
    return merid(merid_coef, flags, field, north, south)


def solution(mesh):
    placed = (P(None, "band", "lon"), P("band", "lon"), P(None, "band", "lon"), P(), P(), P(), P())
    return jax.shard_map(
        on_device, mesh=mesh, in_specs=placed, out_specs=P(None, "band", "lon"), check_vma=False
    )
```

time: 140 us -> 51.9 us (0.37)
  the two profiles are of different devices: /device:TPU:0 before, /device:TPU:28 now
where the time goes in v1:
time: 51.9 us; the launch traced here: 51.6 us
  waiting for transfers between devices  26.7 us (51%)
  Pallas kernels  14.8 us (29%)
  starting transfers between devices  5.7 us (11%)
  local copies, waits for them, and re-layouts  2.88 us (6%)
  between operations  0.79 us (2%)
  other arithmetic  0.62 us (1%)
    ppermute x4, waiting for transfers between devices, turn(): lax.ppermute(value, 'lon', [(i, (i + steps) % count) for i in range(count)])  23.8 us
    pallas_call x1, Pallas kernels, zonal(): pl.pallas_call(functools.partial(zonal_kernel, frame=frame, par_cols=par_...  5.74 us
    pallas_call x1, Pallas kernels, restrict(): pl.pallas_call(functools.partial(restrict_kernel, blocks=blocks, nest_wid...  4.42 us
    ppermute x4, starting transfers between devices, turn(): lax.ppermute(value, 'lon', [(i, (i + steps) % count) for i in range(count)])  4.21 us
    ppermute x1, waiting for transfers between devices, on_device(): other = lax.ppermute(edges[0], 'band', [(0, 1), (1, 0)])  2.92 us
    pallas_call x1, Pallas kernels, merid(): pl.pallas_call(functools.partial(merid_kernel, levels=levels, par_rows=pa...  2.87 us
    pallas_call x1, Pallas kernels, parent_edges(): pl.pallas_call(functools.partial(edges_kernel, par_cols=par_cols), grid=(...  1.81 us
    ppermute x1, starting transfers between devices, on_device(): other = lax.ppermute(edges[0], 'band', [(0, 1), (1, 0)])  1.49 us
  transfers between devices with their start and end apart: 5, of which 2 were waited for; matrix products, arithmetic and copies ran while one was open for 4% of the time, Pallas kernels for 9%

profile of v1, /device:TPU:28, one launch (start us, length us, event | category | flops | bytes accessed | tf_op | source)
XLA Modules:
  0.0 51.6 jit_solution(6238810577436015330)
XLA Ops:
  0.0 1.8 %edges.1 = (f32[8,512]{1,0:T(8,128)}, f32[8,512]{1,0:T(8,128)}) custom-call(f32[32,16,192]{2,1,0:T(8,128)} %parent_ref.1, f32[32,16,192]{2,1,0:T(8,128)} %parent_ref.1), custom_call_target="tpu_custom_call" | custom-call | tf_op jit(solution)/shard_map/edges/pallas_call | solution.py:175
  1.8 0.0 collective-permute-start.192
  1.8 1.7 %collective-permute-start.193 = (f32[8,512]{1,0:T(8,128)}, f32[8,512]{1,0:T(8,128)S(1)}, u32[]{:S(2)}, u32[]{:S(2)}) collective-permute-start(f32[8,512]{1,0:T(8,128)} %get-tuple-element.982), channel_id=1, source_target_pairs={{0,30},{2,0},{4,2},{6,4},{8,6},{10,8},{12,10},{14,12},{16,14},{18,... | collective-permute-start | bytes 49160 | tf_op jit(solution)/shard_map/ppermute | solution.py:342
  4.3 4.4 %restrict.1 = (f32[208,512]{1,0:T(8,128)S(1)}, f32[208,512]{1,0:T(8,128)S(1)}, f32[16,512]{1,0:T(8,128)S(1)}, f32[16,512]{1,0:T(8,128)S(1)}) custom-call(s32[1]{0:T(128)S(6)} %copy.200.offset_ref, f32[32,48,576]{2,1,0:T(8,128)} %refs_4_.1, f32[32,48,576]{2,1,0:T(8,128)} %refs_4_.1, f32[32,48,576]{2,1,0:T(8,128)} %refs_4_.1, f32[32,48,576]{2,1,0:T(8,128)} %refs_4_.1, ...), custom_call_target="tpu_custom_call" | custom-call | tf_op jit(solution)/shard_map/restrict/pallas_call | solution.py:136
  8.7 28.0 %conditional.1 = (f32[208,512]{1,0:T(8,128)}, f32[208,512]{1,0:T(8,128)}) conditional(s32[]{:T(128)} %clamp.3, (f32[208,512]{1,0:T(8,128)S(1)}, f32[16,512]{1,0:T(8,128)S(1)}, f32[208,512]{1,0:T(8,128)S(1)}) %tuple.453, (f32[208,512]{1,0:T(8,128)S(1)}, f32[208,512]{1,0:T(8,128)S(1)}) %tuple.454, ...), branch_computations={%region_0.1_spmd, %region_1.2_spmd, %region_2.3_spmd, %region_3.4_... | conditional | flops 8192 | bytes 4522088 | solution.py:386
  8.8 0.1 collective-permute-start.42
  8.9 2.4 %collective-permute-start.43 = (f32[88,512]{1,0:T(8,128)S(1)}, f32[88,512]{1,0:T(8,128)S(1)}, u32[]{:S(2)}, u32[]{:S(2)}) collective-permute-start(f32[88,512]{1,0:T(8,128)S(1)} %slice.905), channel_id=1, source_target_pairs={{0,16},{2,18},{4,20},{6,22},{8,24},{10,26},{12,28},{14,30},{16,0},... | collective-permute-start | bytes 540680 | tf_op jit(solution)/shard_map/cond/branch_36_fun/ppermute | solution.py:342
  11.3 23.8 %collective-permute-done.43 = f32[88,512]{1,0:T(8,128)S(1)} collective-permute-done((f32[88,512]{1,0:T(8,128)S(1)}, f32[88,512]{1,0:T(8,128)S(1)}, u32[]{:S(2)}, u32[]{:S(2)}) %collective-permute-start.43) | collective-permute-done | bytes 180256 | tf_op jit(solution)/shard_map/cond/branch_36_fun/ppermute | solution.py:342
  35.1 0.8 %pad.386 = f32[208,512]{1,0:T(8,128)} pad(f32[88,512]{1,0:T(8,128)S(1)} %collective-permute-done.43, f32[]{:T(128)} %constant.1127.clone), padding=0_120x0_0 | pad | bytes 606212 | tf_op jit(solution)/shard_map/cond/branch_36_fun/jit(_pad)/pad | solution.py:376
  35.9 0.0 collective-permute-done.42
  35.9 0.8 %pad.385 = f32[208,512]{1,0:T(8,128)} pad(f32[168,512]{1,0:T(8,128)S(1)} %collective-permute-done.42, f32[]{:T(128)} %constant.1127.clone), padding=40_0x0_0 | pad | bytes 770052 | tf_op jit(solution)/shard_map/cond/branch_36_fun/jit(_pad)/pad | solution.py:375
  36.7 0.0 collective-permute-done.192.low_ref
  36.7 0.0 copy-start.1
  36.7 0.0 collective-permute-done.193.high_ref
  36.8 0.0 copy-start.2
  36.8 0.6 %copy-done.1 = f32[8,512]{1,0:T(8,128)} copy-done((f32[8,512]{1,0:T(8,128)}, f32[8,512]{1,0:T(8,128)S(1)}, u32[]{:S(2)}) %copy-start.1) | copy-done | bytes 16408
  37.3 0.0 copy-done.2
  37.4 5.7 %zonal.1 = (f32[32,16,192]{2,1,0:T(8,128)}, f32[96,256]{1,0:T(8,128)}) custom-call(f32[32]{0:T(128)} %relax_ref.1, f32[32]{0:T(128)} %zonal_ref.1, s32[1]{0:T(128)} %bitcast.2.band_ref, f32[208,512]{1,0:T(8,128)} %get-tuple-element.979.near_ref, f32[208,512]{1,0:T(8,128)} %get-tuple-element.980.far_ref, f32[8,512]{1,0:T(8,128)} %copy-done.1, ...), custom_call_target="tpu_custom_call" | custom-call | tf_op jit(solution)/shard_map/zonal/pallas_call | solution.py:258
  43.1 1.5 %collective-permute-start.194 = (f32[96,256]{1,0:T(8,128)}, f32[96,256]{1,0:T(8,128)S(1)}, u32[]{:S(2)}, u32[]{:S(2)}) collective-permute-start(f32[96,256]{1,0:T(8,128)} %get-tuple-element.984), channel_id=1, source_target_pairs={{0,1},{1,0},{2,3},{3,2},{4,5},{5,4},{6,7},{7,6},{8,9},{9,8},{10,11... | collective-permute-start | bytes 294920 | tf_op jit(solution)/shard_map/ppermute | solution.py:396
  44.6 0.6 %add_convert_fusion.flag_ref = s32[2]{0:T(128)} fusion(pred[1]{0:T(512)(128)(4,1)} %bitcast.1, pred[1]{0:T(512)(128)(4,1)} %bitcast), kind=kLoop, calls=%fused_computation.64 | loop fusion | flops 4 | bytes 10 | tf_op jit(solution)/shard_map/convert_element_type | solution.py:401
  45.2 2.9 %collective-permute-done.194.before_ref.after_ref = f32[96,256]{1,0:T(8,128)S(1)} collective-permute-done((f32[96,256]{1,0:T(8,128)}, f32[96,256]{1,0:T(8,128)S(1)}, u32[]{:S(2)}, u32[]{:S(2)}) %collective-permute-start.194) | collective-permute-done | bytes 98336 | tf_op jit(solution)/shard_map/ppermute | solution.py:396
  48.1 0.0 copy-start
  48.1 0.6 %copy-done = f32[96,256]{1,0:T(8,128)} copy-done((f32[96,256]{1,0:T(8,128)}, f32[96,256]{1,0:T(8,128)S(1)}, u32[]{:S(2)}) %copy-start) | copy-done | bytes 98328
  48.8 2.9 %merid.1 = f32[32,16,192]{2,1,0:T(8,128)} custom-call(f32[32]{0:T(128)} %coef_ref.1, s32[2]{0:T(128)} %add_convert_fusion.flag_ref, f32[32,16,192]{2,1,0:T(8,128)} %get-tuple-element.983.field_ref, f32[96,256]{1,0:T(8,128)} %copy-done, f32[96,256]{1,0:T(8,128)} %copy-done), custom_call_target="tpu_custom_call" | custom-call | tf_op jit(solution)/shard_map/merid/pallas_call | solution.py:330
  (2 shorter events, 0.0 us)
Async XLA Ops:
  1.8 34.9 %collective-permute-start.192 = (f32[8,512]{1,0:T(8,128)}, f32[8,512]{1,0:T(8,128)S(1)}, u32[]{:S(2)}, u32[]{:S(2)}) collective-permute-start(f32[8,512]{1,0:T(8,128)} %get-tuple-element.981), channel_id=1, source_target_pairs={{0,2},{2,4},{4,6},{6,8},{8,10},{10,12},{12,14},{14,16},{16,18},{18... | collective-permute-start | bytes 49160 | tf_op jit(solution)/shard_map/ppermute | solution.py:342
  1.8 34.9 %collective-permute-start.193 = (f32[8,512]{1,0:T(8,128)}, f32[8,512]{1,0:T(8,128)S(1)}, u32[]{:S(2)}, u32[]{:S(2)}) collective-permute-start(f32[8,512]{1,0:T(8,128)} %get-tuple-element.982), channel_id=1, source_target_pairs={{0,30},{2,0},{4,2},{6,4},{8,6},{10,8},{12,10},{14,12},{16,14},{18,... | collective-permute-start | bytes 49160 | tf_op jit(solution)/shard_map/ppermute | solution.py:342
  8.8 27.1 %collective-permute-start.42 = (f32[168,512]{1,0:T(8,128)S(1)}, f32[168,512]{1,0:T(8,128)S(1)}, u32[]{:S(2)}, u32[]{:S(2)}) collective-permute-start(f32[168,512]{1,0:T(8,128)S(1)} %slice.904), channel_id=1, source_target_pairs={{0,14},{2,16},{4,18},{6,20},{8,22},{10,24},{12,26},{14,28},{16,30}... | collective-permute-start | bytes 1032200 | tf_op jit(solution)/shard_map/cond/branch_36_fun/ppermute | solution.py:342
  8.9 26.2 %collective-permute-start.43 = (f32[88,512]{1,0:T(8,128)S(1)}, f32[88,512]{1,0:T(8,128)S(1)}, u32[]{:S(2)}, u32[]{:S(2)}) collective-permute-start(f32[88,512]{1,0:T(8,128)S(1)} %slice.905), channel_id=1, source_target_pairs={{0,16},{2,18},{4,20},{6,22},{8,24},{10,26},{12,28},{14,30},{16,0},... | collective-permute-start | bytes 540680 | tf_op jit(solution)/shard_map/cond/branch_36_fun/ppermute | solution.py:342
  36.7 0.6 %copy-start.1 = (f32[8,512]{1,0:T(8,128)}, f32[8,512]{1,0:T(8,128)S(1)}, u32[]{:S(2)}) copy-start(f32[8,512]{1,0:T(8,128)S(1)} %collective-permute-done.192.low_ref) | copy-start | bytes 49156
  36.8 0.6 %copy-start.2 = (f32[8,512]{1,0:T(8,128)}, f32[8,512]{1,0:T(8,128)S(1)}, u32[]{:S(2)}) copy-start(f32[8,512]{1,0:T(8,128)S(1)} %collective-permute-done.193.high_ref) | copy-start | bytes 49156
  43.1 5.0 %collective-permute-start.194 = (f32[96,256]{1,0:T(8,128)}, f32[96,256]{1,0:T(8,128)S(1)}, u32[]{:S(2)}, u32[]{:S(2)}) collective-permute-start(f32[96,256]{1,0:T(8,128)} %get-tuple-element.984), channel_id=1, source_target_pairs={{0,1},{1,0},{2,3},{3,2},{4,5},{5,4},{6,7},{7,6},{8,9},{9,8},{10,11... | collective-permute-start | bytes 294920 | tf_op jit(solution)/shard_map/ppermute | solution.py:396
  48.1 0.6 %copy-start = (f32[96,256]{1,0:T(8,128)}, f32[96,256]{1,0:T(8,128)S(1)}, u32[]{:S(2)}) copy-start(f32[96,256]{1,0:T(8,128)S(1)} %collective-permute-done.194.before_ref.after_ref) | copy-start | bytes 294916
